TPU v7x, 32 devices: a whole 2x2x4 slice. The times are simulated.
32 devices in a mesh: expert: 4 (over y, core), shard: 8 (over z, x).
Axes of the slice: x: 2, y: 2, z: 4, core: 2. Of those that a mesh axis runs over, the one named last changes fastest.
Arguments:
- params: float32 [3, 4, 6144, 256], P(None, 'expert', 'shard'), may hold values from -3 to 3
- grads: float32 [3, 4, 6144, 256], P(None, 'expert', 'shard')
- moment: float32 [3, 4, 6144, 256], P(None, 'expert', 'shard'), may hold values from -0.6 to 0.6
- second: float32 [3, 4, 64], P(None, 'expert'), may hold values from 0.002 to 0.2
- step: int32 [1], replicated, may hold values from 1 to 8
- block_map: int32 [256], replicated, may hold values from 0 to 63, never falling along the last dimension, each value on 1 to 8 neighbouring positions
Outputs:
- new_weights: bfloat16 [3, 4, 6144, 256], P(None, 'expert')
- new_moment: float32 [3, 4, 6144, 256], P(None, 'expert', 'shard')
- new_second: float32 [3, 4, 64], P(None, 'expert')
Inputs may be any that keep to these rules, and one draw needn't show every extreme that they name: `block_map`: every block holds at least one neuron and at most 8.
All inputs are finite; a program needn't handle non-finite values.
Results may differ from a plain program's by a relative error of at most 0.001.
Values may be sent and summed in bfloat16 or wider, within the bound.
A program may use at most 64 MiB of HBM per device.

v0:
```python
import functools
import math

import jax
import jax.numpy as jnp
from jax import lax
from jax.experimental import pallas as pl
from jax.experimental.pallas import tpu as pltpu
from jax.sharding import PartitionSpec as P

LEARN_RATE = 0.05
DECAY_WEIGHT = 0.1
BETA_FIRST = 0.9
BETA_SECOND = 0.95
epsilon = 1e-08
MESH = pl.DeviceIdType.MESH
LANES = 128
STRIP = 64


def ring_position(shard, n):
    if n % 2:
        return shard
    row, side = shard // 2, shard % 2
    return jnp.where(side == 0, row, n - 1 - row)


def ring_shard(position, n):
    position = lax.rem(position + 2 * n, n)
    if n % 2:
        return position
    return jnp.where(position < n // 2, 2 * position, 2 * (n - 1 - position) + 1)


def kernel(
    experts,
    shards,
    limit,
    params,
    grads,
    moment,
    second,
    step,
    block_map,
    weights,
    new_moment,
    new_second,
    p_buf,
    g_buf,
    m_buf,
    s_buf,
    map_buf,
    tile,
    total_row,
    tiles,
    totals,
    load_sem,
    small_sem,
    tile_send,
    tile_recv,
    total_send,
    total_recv,
    ring_send,
    ring_recv,
):
    e = lax.axis_index("expert")
    s = lax.axis_index("shard")
    devices = experts * shards
    me = e * shards + s
    mats, rows, neurons = p_buf.shape
    width = rows * shards
    folds = neurons // LANES

    for k in range(mats):
        pltpu.make_async_copy(grads.at[k], g_buf.at[k], load_sem.at[0, k]).start()
    for k in range(mats):
        pltpu.make_async_copy(moment.at[k], m_buf.at[k], load_sem.at[1, k]).start()
        pltpu.make_async_copy(params.at[k], p_buf.at[k], load_sem.at[2, k]).start()

    map_load = pltpu.make_async_copy(block_map, map_buf, small_sem.at[0])
    second_load = pltpu.make_async_copy(second, s_buf, small_sem.at[1])
    map_load.start()
    second_load.start()

    barrier = pltpu.get_barrier_semaphore()

    def greet(j, carry):
        other = lax.rem(me + j, devices)
        pl.semaphore_signal(
            barrier,
            inc=1,
            device_id=(other // shards, lax.rem(other, shards)),
            device_id_type=MESH,
        )
        return carry

    lax.fori_loop(1, devices, greet, 0)

    blocks = second.shape[2]
    map_load.wait()
    second_load.wait()
    table = (
        lax.broadcasted_iota(jnp.int32, (blocks, neurons), 0) == map_buf[...]
    ).astype(jnp.float32)
    members = lax.dot_general(
        jnp.ones((8, neurons), jnp.float32),
        table,
        (((1,), (1,)), ((), ())),
        precision=lax.Precision.HIGHEST,
    )[:mats]
    step_value = jnp.full((1, LANES), step[0].astype(jnp.float32))
    first_fix = 1.0 - jnp.power(jnp.full((1, LANES), BETA_FIRST, jnp.float32), step_value)
    second_fix = 1.0 - jnp.power(jnp.full((1, LANES), BETA_SECOND, jnp.float32), step_value)
    first_fix = first_fix[:, :1]
    second_fix = second_fix[:, :1]

    squares = []
    for k in range(mats):
        pltpu.make_async_copy(grads.at[k], g_buf.at[k], load_sem.at[0, k]).wait()

        def add_squares(i, acc, k=k):
            g = g_buf[k, pl.ds(pl.multiple_of(i * STRIP, STRIP), STRIP), :]
            return acc + jnp.sum((g * g).reshape(STRIP // 8, 8, neurons), axis=0)

        acc = lax.fori_loop(0, rows // STRIP, add_squares, jnp.zeros((8, neurons), jnp.float32), unroll=2)
        squares.append(jnp.sum(acc, axis=0, keepdims=True))
    parts = [sq[:, f * LANES : (f + 1) * LANES] for f in range(folds) for sq in squares]
    own_total = functools.reduce(lambda a, b: a + b, parts)
    own_total = jnp.broadcast_to(jnp.sum(own_total, axis=1, keepdims=True), (1, LANES))
    pad = tile.shape[0] - len(parts)
    if pad:
        parts.append(jnp.zeros((pad, LANES), jnp.float32))
    own_tile = jnp.concatenate(parts, axis=0)
    tile[...] = own_tile
    total_row[...] = own_total
    tiles[s] = own_tile
    totals[me] = own_total

    pl.semaphore_wait(barrier, devices - 1)

    def tile_copy(j, arriving):
        to = lax.rem(s + j, shards)
        origin = lax.rem(s + shards - j, shards) if arriving else s
        return pltpu.make_async_remote_copy(
            src_ref=tile,
            dst_ref=tiles.at[origin],
            send_sem=tile_send.at[j],
            recv_sem=tile_recv.at[j],
            device_id=(e, to),
            device_id_type=MESH,
        )

    def total_copy(j, arriving):
        other = lax.rem(me + j, devices)
        origin = lax.rem(me + devices - j, devices) if arriving else me
        return pltpu.make_async_remote_copy(
            src_ref=total_row,
            dst_ref=totals.at[origin],
            send_sem=total_send.at[j],
            recv_sem=total_recv.at[j],
            device_id=(other // shards, lax.rem(other, shards)),
            device_id_type=MESH,
        )

    def start_total(j, carry):
        total_copy(j, False).start()
        return carry

    def start_tile(j, carry):
        tile_copy(j, False).start()
        return carry

    def wait_total(j, carry):
        total_copy(j, True).wait_recv()
        return carry

    def wait_tile(j, carry):
        tile_copy(j, True).wait_recv()
        return carry

    def sent_total(j, carry):
        total_copy(j, False).wait_send()
        return carry

    def sent_tile(j, carry):
        tile_copy(j, False).wait_send()
        return carry

    lax.fori_loop(1, devices, start_total, 0)
    lax.fori_loop(1, shards, start_tile, 0)
    lax.fori_loop(1, devices, wait_total, 0)
    lax.fori_loop(1, shards, wait_tile, 0)

    total = jnp.sum(totals[...], axis=0)
    clip = jnp.minimum(1.0, limit / (jnp.sqrt(total) + 1e-06))[:, :1]
    all_tile = jnp.sum(tiles[...], axis=0)
    square = jnp.concatenate(
        [all_tile[f * mats : (f + 1) * mats] for f in range(folds)], axis=1
    )
    block_sums = lax.dot_general(
        square, table, (((1,), (1,)), ((), ())), precision=lax.Precision.HIGHEST
    )
    updated = BETA_SECOND * s_buf[:, 0, :] + (1.0 - BETA_SECOND) * clip * clip * block_sums / (
        width * members
    )
    for k in range(mats):
        new_second[k] = updated[k : k + 1]
    divisor = jnp.sqrt(updated / second_fix) + epsilon
    by_neuron = lax.dot_general(
        divisor, table, (((1,), (0,)), ((), ())), precision=lax.Precision.HIGHEST
    )
    rate = LEARN_RATE / (first_fix * by_neuron)
    grad_scale = (1.0 - BETA_FIRST) * clip

    place = ring_position(s, shards)
    half = rows // 2
    right = ring_shard(place + 1, shards)
    left = ring_shard(place - 1, shards)
    far, near = shards // 2, (shards - 1) // 2
    hops = ((far, near), (near, far))

    def ring_copy(way, hop, k, part, arriving):
        back = hop + (1 if arriving else 0)
        origin = ring_shard(place - back if way == 0 else place + back, shards)
        block = weights.at[k, pl.ds(pl.multiple_of(origin * rows + part * half, half), half), :]
        return pltpu.make_async_remote_copy(
            src_ref=block,
            dst_ref=block,
            send_sem=ring_send.at[way, hop, 2 * k + part],
            recv_sem=ring_recv.at[way, hop, 2 * k + part],
            device_id=(e, right if way == 0 else left),
            device_id_type=MESH,
        )

    for k in range(mats):
        pltpu.make_async_copy(moment.at[k], m_buf.at[k], load_sem.at[1, k]).wait()
        pltpu.make_async_copy(params.at[k], p_buf.at[k], load_sem.at[2, k]).wait()
        rate_k = rate[k : k + 1]
        for part in range(2):

            def update(i, carry, k=k, part=part, rate_k=rate_k):
                at = pl.multiple_of(part * half + i * STRIP, STRIP)
                strip = pl.ds(at, STRIP)
                value = BETA_FIRST * m_buf[k, strip, :] + grad_scale * g_buf[k, strip, :]
                new_moment[k, strip, :] = value
                out = p_buf[k, strip, :] * (1.0 - LEARN_RATE * DECAY_WEIGHT) - rate_k * value
                weights[k, pl.ds(pl.multiple_of(s * rows + at, STRIP), STRIP), :] = out.astype(
                    jnp.bfloat16
                )
                return carry

            lax.fori_loop(0, half // STRIP, update, 0, unroll=2)
            for way in range(2):
                if hops[way][part] > 0:
                    ring_copy(way, 0, k, part, False).start()

    for hop in range(far):
        for k in range(mats):
            for part in range(2):
                for way in range(2):
                    if hop < hops[way][part]:
                        ring_copy(way, hop, k, part, True).wait_recv()
                        if hop + 1 < hops[way][part]:
                            ring_copy(way, hop + 1, k, part, False).start()
    for hop in range(far):
        for k in range(mats):
            for part in range(2):
                for way in range(2):
                    if hop < hops[way][part]:
                        ring_copy(way, hop, k, part, False).wait_send()
    lax.fori_loop(1, devices, sent_total, 0)
    lax.fori_loop(1, shards, sent_tile, 0)


def store_kernel(weights, moment, second, weights_out, moment_out, second_out, sem):
    mats = weights.shape[0]
    copies = [
        pltpu.make_async_copy(weights.at[k], weights_out.at[k], sem.at[0, k]) for k in range(mats)
    ] + [pltpu.make_async_copy(moment.at[k], moment_out.at[k], sem.at[1, k]) for k in range(mats)]
    copies.append(pltpu.make_async_copy(second, second_out, sem.at[0, mats]))
    for copy in copies:
        copy.start()
    for copy in copies:
        copy.wait()


def body(params, grads, moment, second, step, block_map):
    experts, shards = lax.axis_size("expert"), lax.axis_size("shard")
    mats, own, rows, neurons = params.shape
    blocks = second.shape[2]
    width = rows * shards
    devices = experts * shards
    limit = math.sqrt(mats * experts * own * width * neurons)
    flat = (mats, own * rows, neurons)
    far = max(shards // 2, 1)
    tile_rows = -(-mats * (neurons // LANES) // 8) * 8
    hbm = pl.BlockSpec(memory_space=pltpu.HBM)
    vmem = pl.BlockSpec(memory_space=pltpu.VMEM)
    smem = pl.BlockSpec(memory_space=pltpu.SMEM)
    dma = pltpu.SemaphoreType.DMA
    shapes = (
        jax.ShapeDtypeStruct((mats, width, neurons), jnp.bfloat16),
        jax.ShapeDtypeStruct(flat, jnp.float32),
        jax.ShapeDtypeStruct((mats, own, blocks), jnp.float32),
    )
    results = pl.pallas_call(
        functools.partial(kernel, experts, shards, limit),
        out_shape=tuple(pltpu.VMEM(shape.shape, shape.dtype) for shape in shapes),
        in_specs=[hbm, hbm, hbm, hbm, smem, hbm],
        out_specs=(vmem, vmem, vmem),
        scratch_shapes=[
            pltpu.VMEM(flat, jnp.float32),
            pltpu.VMEM(flat, jnp.float32),
            pltpu.VMEM(flat, jnp.float32),
            pltpu.VMEM((mats, own, blocks), jnp.float32),
            pltpu.VMEM((1, neurons), jnp.int32),
            pltpu.VMEM((tile_rows, LANES), jnp.float32),
            pltpu.VMEM((1, LANES), jnp.float32),
            pltpu.VMEM((shards, tile_rows, LANES), jnp.float32),
            pltpu.VMEM((devices, 1, LANES), jnp.float32),
            dma((3, mats)),
            dma((2,)),
            dma((shards,)),
            dma((shards,)),
            dma((devices,)),
            dma((devices,)),
            dma((2, far, 2 * mats)),
            dma((2, far, 2 * mats)),
        ],
        compiler_params=pltpu.CompilerParams(
            collective_id=0, has_side_effects=True, vmem_limit_bytes=46 * 1024 * 1024
        ),
    )(
        params.reshape(flat),
        grads.reshape(flat),
        moment.reshape(flat),
        second,
        step,
        block_map.reshape(1, neurons),
    )
    weights, new_moment, new_second = pl.pallas_call(
        store_kernel,
        out_shape=shapes,
        in_specs=[vmem, vmem, vmem],
        out_specs=(hbm, hbm, hbm),
        scratch_shapes=[dma((2, mats + 1))],
        compiler_params=pltpu.CompilerParams(vmem_limit_bytes=8 * 1024 * 1024),
    )(*results)
    return (
        weights.reshape(mats, own, width, neurons),
        new_moment.reshape(mats, own, rows, neurons),
        new_second,
    )


def solution(mesh):
    placed = (
        P(None, "expert", "shard", None),
        P(None, "expert", "shard", None),
        P(None, "expert", "shard", None),
        P(None, "expert", None),
        P(),
        P(),
    )
    return jax.shard_map(
        body,
        mesh=mesh,
        in_specs=placed,
        out_specs=(
            P(None, "expert", None, None),
            P(None, "expert", "shard", None),
            P(None, "expert", None),
        ),
        check_vma=False,
    )
```

profile of v0, /device:TPU:0, one launch (start us, length us, event | category | flops | bytes accessed | tf_op | source)
XLA Modules:
  0.0 110.3 jit_solution(6879837908787591249)
XLA Ops:
  1.3 104.5 %shard_map.85 = (bf16[3,6144,256]{2,1,0:T(8,128)(2,1)S(1)}, f32[3,768,256]{2,1,0:T(8,128)S(1)}, f32[3,1,64]{2,1,0:T(1,128)S(1)}) custom-call(f32[3,768,256]{2,1,0:T(8,128)} %bitcast.10, f32[3,768,256]{2,1,0:T(8,128)} %bitcast.11, f32[3,768,256]{2,1,0:T(8,128)} %bitcast.12, f32[3,1,64]{2,1,0:T(1,128)} %second.1, s32[1]{0:T(128)S(6)} %copy.11.step, ...), custom_call_target="tpu_custom_call" | custom-call | tf_op jit(solution)/shard_map/pallas_call | solution.py:306
  105.8 4.4 %shard_map.86 = (bf16[3,6144,256]{2,1,0:T(8,128)(2,1)}, f32[3,768,256]{2,1,0:T(8,128)}, f32[3,1,64]{2,1,0:T(1,128)}) custom-call(bf16[3,6144,256]{2,1,0:T(8,128)(2,1)S(1)} %get-tuple-element.9.weights, f32[3,768,256]{2,1,0:T(8,128)S(1)} %get-tuple-element.10.moment, f32[3,1,64]{2,1,0:T(1,128)S(1)} %get-tuple-element.11.second), custom_call_target="tpu_custom_call" | custom-call | tf_op jit(solution)/shard_map/pallas_call | solution.py:341
where the time goes:
time: 110 us
  Pallas kernels  109 us (99%)
  between operations  1.29 us (1%)
    pallas_call x1, Pallas kernels, body(): pl.pallas_call(functools.partial(kernel, experts, shards, limit), out_sha...  105 us
    pallas_call x1, Pallas kernels, body(): pl.pallas_call(store_kernel, out_shape=shapes, in_specs=[vmem, vmem, vmem...  4.44 us

commit v1 on v0

v1 whole, which is shorter than its diff:
```python
import functools
import itertools
import math

import jax
import jax.numpy as jnp
from jax import lax
from jax.experimental import pallas as pl
from jax.experimental.pallas import tpu as pltpu
from jax.sharding import PartitionSpec as P

LEARN_RATE = 0.05
DECAY_WEIGHT = 0.1
BETA_FIRST = 0.9
BETA_SECOND = 0.95
epsilon = 1e-08
MESH = pl.DeviceIdType.MESH
LANES = 128
STRIP = 64
CUTS = 1


def ring_position(shard, n):
    if n % 2:
        return shard
    row, side = shard // 2, shard % 2
    return jnp.where(side == 0, row, n - 1 - row)


def ring_shard(position, n):
    position = lax.rem(position + 2 * n, n)
    if n % 2:
        return position
    return jnp.where(position < n // 2, 2 * position, 2 * (n - 1 - position) + 1)


def split3(x):
    high = x.astype(jnp.bfloat16)
    rest = x - high.astype(jnp.float32)
    middle = rest.astype(jnp.bfloat16)
    low = (rest - middle.astype(jnp.float32)).astype(jnp.bfloat16)
    return jnp.concatenate([high, middle, low], axis=0)


def gather_columns(x, onehot, dims):
    n = x.shape[0]
    out = lax.dot_general(split3(x), onehot, (dims, ((), ())), preferred_element_type=jnp.float32)
    return out[:n] + out[n : 2 * n] + out[2 * n :]


def kernel(
    experts,
    shards,
    limit,
    params,
    grads,
    moment,
    second,
    step,
    block_map,
    weights,
    new_moment,
    new_second,
    g_buf,
    pm_buf,
    s_buf,
    map_buf,
    tile,
    total_row,
    tiles,
    totals,
    load_sem,
    small_sem,
    tile_sem,
    total_sem,
    ring_send,
    ring_recv,
):
    e = lax.axis_index("expert")
    s = lax.axis_index("shard")
    devices = experts * shards
    me = e * shards + s
    mats, rows, neurons = g_buf.shape
    width = rows * shards
    folds = neurons // LANES
    backward = s < shards // 2

    def far_first(t, own, count):
        t = jnp.where(backward, count - 2 - t, t)
        return t + (t >= own).astype(jnp.int32)

    barrier = pltpu.get_barrier_semaphore()

    def greet(t, carry):
        other = far_first(t, me, devices)
        pl.semaphore_signal(
            barrier,
            inc=1,
            device_id=(lax.div(other, shards), lax.rem(other, shards)),
            device_id_type=MESH,
        )
        return carry

    lax.fori_loop(0, devices - 1, greet, 0)

    map_load = pltpu.make_async_copy(block_map, map_buf, small_sem.at[0])
    second_load = pltpu.make_async_copy(second, s_buf, small_sem.at[1])
    for k in range(mats):
        pltpu.make_async_copy(grads.at[k], g_buf.at[k], load_sem.at[k]).start()
    map_load.start()
    second_load.start()

    blocks = second.shape[2]
    map_load.wait()
    own_blocks = map_buf[...]
    table = (
        lax.broadcasted_iota(jnp.int32, (blocks, neurons), 0) == own_blocks
    ).astype(jnp.bfloat16)
    same = lax.dot_general(
        table, table, (((0,), (0,)), ((), ())), preferred_element_type=jnp.float32
    ).astype(jnp.bfloat16)
    members = lax.dot_general(
        jnp.ones((8, neurons), jnp.bfloat16),
        table,
        (((1,), (1,)), ((), ())),
        preferred_element_type=jnp.float32,
    )[:mats]
    members_here = lax.dot_general(
        jnp.ones((8, neurons), jnp.bfloat16),
        same,
        (((1,), (0,)), ((), ())),
        preferred_element_type=jnp.float32,
    )[:mats]
    second_load.wait()
    second_here = gather_columns(s_buf[:, 0, :], table, ((1,), (0,)))
    step_value = jnp.full((1, LANES), step[0].astype(jnp.float32))
    first_fix = 1.0 - jnp.power(jnp.full((1, LANES), BETA_FIRST, jnp.float32), step_value)
    second_fix = 1.0 - jnp.power(jnp.full((1, LANES), BETA_SECOND, jnp.float32), step_value)
    first_fix = first_fix[:, :1]
    second_fix = second_fix[:, :1]

    squares = []
    for k in range(mats):
        pltpu.make_async_copy(grads.at[k], g_buf.at[k], load_sem.at[k]).wait()
        if k == mats - 1:
            for i in range(mats):
                pltpu.make_async_copy(params.at[i], pm_buf.at[0, i], load_sem.at[mats + i]).start()
                pltpu.make_async_copy(moment.at[i], pm_buf.at[1, i], load_sem.at[mats + i]).start()

        def add_squares(i, acc, k=k):
            g = g_buf[k, pl.ds(pl.multiple_of(i * STRIP, STRIP), STRIP), :]
            return acc + jnp.sum((g * g).reshape(STRIP // 8, 8, neurons), axis=0)

        acc = lax.fori_loop(0, rows // STRIP, add_squares, jnp.zeros((8, neurons), jnp.float32), unroll=2)
        squares.append(jnp.sum(acc, axis=0, keepdims=True))
    parts = [sq[:, f * LANES : (f + 1) * LANES] for f in range(folds) for sq in squares]
    own_total = functools.reduce(lambda a, b: a + b, parts)
    pad = tile.shape[0] - len(parts)
    if pad:
        parts.append(jnp.zeros((pad, LANES), jnp.float32))
    own_tile = jnp.concatenate(parts, axis=0)
    tile[...] = own_tile
    total_row[...] = own_total
    tiles[s] = own_tile

    def blank(i, carry):
        totals[e * shards + i] = jnp.zeros((1, LANES), jnp.float32)
        return carry

    lax.fori_loop(0, shards, blank, 0)

    pl.semaphore_wait(barrier, devices - 1)

    def start_total(t, carry):
        other_s = jnp.where(backward, shards - 1 - t, t)
        for d in range(1, experts):
            pltpu.make_async_remote_copy(
                src_ref=total_row,
                dst_ref=totals.at[me],
                send_sem=total_sem.at[0],
                recv_sem=total_sem.at[1],
                device_id=(lax.rem(e + d, experts), other_s),
                device_id_type=MESH,
            ).start()
        return carry

    def start_tile(t, carry):
        pltpu.make_async_remote_copy(
            src_ref=tile,
            dst_ref=tiles.at[s],
            send_sem=tile_sem.at[0],
            recv_sem=tile_sem.at[1],
            device_id=(e, far_first(t, s, shards)),
            device_id_type=MESH,
        ).start()
        return carry

    def wait_bytes(ref, sem):
        pltpu.make_async_copy(ref, ref, sem).wait()

    lax.fori_loop(0, shards, start_total, 0)
    lax.fori_loop(0, shards - 1, start_tile, 0)
    other_tiles = tiles.at[pl.ds(0, shards - 1)]
    other_totals = totals.at[pl.ds(0, devices - shards)]
    wait_bytes(other_tiles, tile_sem.at[1])
    wait_bytes(other_totals, total_sem.at[1])

    all_tile = jnp.sum(tiles[...], axis=0)
    total = jnp.sum(totals[...], axis=0) + jnp.sum(all_tile, axis=0, keepdims=True)
    total = jnp.sum(total, axis=1, keepdims=True)
    square = jnp.concatenate(
        [all_tile[f * mats : (f + 1) * mats] for f in range(folds)], axis=1
    )
    sums_here = gather_columns(square, same, ((1,), (0,)))
    clip = jnp.minimum(1.0, limit / (jnp.sqrt(total) + 1e-06))
    updated_here = BETA_SECOND * second_here + (1.0 - BETA_SECOND) * clip * clip * sums_here / (
        width * members_here
    )
    by_neuron = jnp.sqrt(updated_here / second_fix) + epsilon
    rate = LEARN_RATE / (first_fix * by_neuron)
    grad_scale = (1.0 - BETA_FIRST) * clip

    place = ring_position(s, shards)
    half = rows // 2
    right = ring_shard(place + 1, shards)
    left = ring_shard(place - 1, shards)
    far, near = shards // 2, (shards - 1) // 2
    hops = ((far, near), (near, far))

    piece = half // CUTS

    def ring_copy(way, hop, part, k, q, arriving):
        back = hop + (1 if arriving else 0)
        origin = ring_shard(place - back if way == 0 else place + back, shards)
        first = pl.multiple_of(origin * rows + part * half + q * piece, piece)
        block = weights.at[k, pl.ds(first, piece), :]
        index = ((2 * hop + part) * mats + k) * CUTS + q
        return pltpu.make_async_remote_copy(
            src_ref=block,
            dst_ref=block,
            send_sem=ring_send,
            recv_sem=ring_recv.at[way, index],
            device_id=(e, right if way == 0 else left),
            device_id_type=MESH,
        )

    for k in range(mats):
        wait_bytes(pm_buf.at[:, k], load_sem.at[mats + k])
        rate_k = rate[k : k + 1]
        for part in range(2):
            for q in range(CUTS):

                def update(i, carry, k=k, part=part, q=q, rate_k=rate_k):
                    at = pl.multiple_of(part * half + q * piece + i * STRIP, STRIP)
                    strip = pl.ds(at, STRIP)
                    value = BETA_FIRST * pm_buf[1, k, strip, :] + grad_scale * g_buf[k, strip, :]
                    new_moment[k, strip, :] = value
                    out = pm_buf[0, k, strip, :] * (1.0 - LEARN_RATE * DECAY_WEIGHT) - rate_k * value
                    weights[k, pl.ds(pl.multiple_of(s * rows + at, STRIP), STRIP), :] = out.astype(
                        jnp.bfloat16
                    )
                    return carry

                lax.fori_loop(0, piece // STRIP, update, 0, unroll=2)
                for way in range(2):
                    if hops[way][part] > 0:
                        ring_copy(way, 0, part, k, q, False).start()

    block_sums = gather_columns(square, table, ((1,), (1,)))
    updated = BETA_SECOND * s_buf[:, 0, :] + (1.0 - BETA_SECOND) * clip * clip * block_sums / (
        width * members
    )
    for k in range(mats):
        new_second[k] = updated[k : k + 1]

    for hop in range(far):
        for k, part, q in itertools.product(range(mats), range(2), range(CUTS)):
            for way in range(2):
                if hop < hops[way][part]:
                    ring_copy(way, hop, part, k, q, True).wait_recv()
                    if hop + 1 < hops[way][part]:
                        ring_copy(way, hop + 1, part, k, q, False).start()
    wait_bytes(weights.at[:, pl.ds(0, width - rows), :], ring_send)
    wait_bytes(other_tiles, tile_sem.at[0])
    wait_bytes(other_totals, total_sem.at[0])


def store_kernel(weights, moment, second, weights_out, moment_out, second_out, sem):
    mats = weights.shape[0]
    for k in range(mats):
        pltpu.make_async_copy(weights.at[k], weights_out.at[k], sem.at[0]).start()
    for k in range(mats):
        pltpu.make_async_copy(moment.at[k], moment_out.at[k], sem.at[1]).start()
    second_copy = pltpu.make_async_copy(second, second_out, sem.at[2])
    second_copy.start()
    pltpu.make_async_copy(weights, weights_out, sem.at[0]).wait()
    pltpu.make_async_copy(moment, moment_out, sem.at[1]).wait()
    second_copy.wait()


def body(params, grads, moment, second, step, block_map):
    experts, shards = lax.axis_size("expert"), lax.axis_size("shard")
    mats, own, rows, neurons = params.shape
    blocks = second.shape[2]
    width = rows * shards
    devices = experts * shards
    limit = math.sqrt(mats * experts * own * width * neurons)
    flat = (mats, own * rows, neurons)
    far = max(shards // 2, 1)
    tile_rows = -(-mats * (neurons // LANES) // 8) * 8
    hbm = pl.BlockSpec(memory_space=pltpu.HBM)
    vmem = pl.BlockSpec(memory_space=pltpu.VMEM)
    smem = pl.BlockSpec(memory_space=pltpu.SMEM)
    dma = pltpu.SemaphoreType.DMA
    shapes = (
        jax.ShapeDtypeStruct((mats, width, neurons), jnp.bfloat16),
        jax.ShapeDtypeStruct(flat, jnp.float32),
        jax.ShapeDtypeStruct((mats, own, blocks), jnp.float32),
    )
    results = pl.pallas_call(
        functools.partial(kernel, experts, shards, limit),
        out_shape=tuple(pltpu.VMEM(shape.shape, shape.dtype) for shape in shapes),
        in_specs=[hbm, hbm, hbm, hbm, smem, hbm],
        out_specs=(vmem, vmem, vmem),
        scratch_shapes=[
            pltpu.VMEM(flat, jnp.float32),
            pltpu.VMEM((2, *flat), jnp.float32),
            pltpu.VMEM((mats, own, blocks), jnp.float32),
            pltpu.VMEM((1, neurons), jnp.int32),
            pltpu.VMEM((tile_rows, LANES), jnp.float32),
            pltpu.VMEM((1, LANES), jnp.float32),
            pltpu.VMEM((shards, tile_rows, LANES), jnp.float32),
            pltpu.VMEM((devices, 1, LANES), jnp.float32),
            dma((2 * mats,)),
            dma((2,)),
            dma((2,)),
            dma((2,)),
            dma(()),
            dma((2, 2 * far * mats * CUTS)),
        ],
        compiler_params=pltpu.CompilerParams(
            collective_id=0, has_side_effects=True, vmem_limit_bytes=46 * 1024 * 1024
        ),
    )(
        params.reshape(flat),
        grads.reshape(flat),
        moment.reshape(flat),
        second,
        step,
        block_map.reshape(1, neurons),
    )
    weights, new_moment, new_second = pl.pallas_call(
        store_kernel,
        out_shape=shapes,
        in_specs=[vmem, vmem, vmem],
        out_specs=(hbm, hbm, hbm),
        scratch_shapes=[dma((3,))],
        compiler_params=pltpu.CompilerParams(vmem_limit_bytes=8 * 1024 * 1024),
    )(*results)
    return (
        weights.reshape(mats, own, width, neurons),
        new_moment.reshape(mats, own, rows, neurons),
        new_second,
    )


def solution(mesh):
    placed = (
        P(None, "expert", "shard", None),
        P(None, "expert", "shard", None),
        P(None, "expert", "shard", None),
        P(None, "expert", None),
        P(),
        P(),
    )
    return jax.shard_map(
        body,
        mesh=mesh,
        in_specs=placed,
        out_specs=(
            P(None, "expert", None, None),
            P(None, "expert", "shard", None),
            P(None, "expert", None),
        ),
        check_vma=False,
    )
```

time: 110 us -> 107 us (0.973)
  Pallas kernels: 109 us -> 106 us
    pallas_call x1, Pallas kernels: 105 us -> 102 us  [body(): pl.pallas_call(functools.partial(kernel, experts, shards, limit), out_sha...]
where the time goes in v1:
time: 107 us
  Pallas kernels  106 us (99%)
  between operations  1.29 us (1%)
    pallas_call x1, Pallas kernels, body(): pl.pallas_call(functools.partial(kernel, experts, shards, limit), out_sha...  102 us
    pallas_call x1, Pallas kernels, body(): pl.pallas_call(store_kernel, out_shape=shapes, in_specs=[vmem, vmem, vmem...  4.4 us

profile of v1, /device:TPU:0, one launch (start us, length us, event | category | flops | bytes accessed | tf_op | source)
XLA Modules:
  0.0 107.3 jit_solution(5760234481618183839)
XLA Ops:
  1.3 101.6 %shard_map.85 = (bf16[3,6144,256]{2,1,0:T(8,128)(2,1)S(1)}, f32[3,768,256]{2,1,0:T(8,128)S(1)}, f32[3,1,64]{2,1,0:T(1,128)S(1)}) custom-call(f32[3,768,256]{2,1,0:T(8,128)} %bitcast.10, f32[3,768,256]{2,1,0:T(8,128)} %bitcast.11, f32[3,768,256]{2,1,0:T(8,128)} %bitcast.12, f32[3,1,64]{2,1,0:T(1,128)} %second.1, s32[1]{0:T(128)S(6)} %copy.11.step, ...), custom_call_target="tpu_custom_call" | custom-call | tf_op jit(solution)/shard_map/pallas_call | solution.py:320
  102.9 4.4 %shard_map.86 = (bf16[3,6144,256]{2,1,0:T(8,128)(2,1)}, f32[3,768,256]{2,1,0:T(8,128)}, f32[3,1,64]{2,1,0:T(1,128)}) custom-call(bf16[3,6144,256]{2,1,0:T(8,128)(2,1)S(1)} %get-tuple-element.9.weights, f32[3,768,256]{2,1,0:T(8,128)S(1)} %get-tuple-element.10.moment, f32[3,1,64]{2,1,0:T(1,128)S(1)} %get-tuple-element.11.second), custom_call_target="tpu_custom_call" | custom-call | tf_op jit(solution)/shard_map/pallas_call | solution.py:352
